TPU v7x, 32 devices: a whole 2x2x4 slice. The times are simulated.
32 devices in a mesh: rep: 2 (over y), gx: 8 (over z, x), gy: 2 (over core).
Axes of the slice: x: 2, y: 2, z: 4, core: 2. Of those that a mesh axis runs over, the one named last changes fastest.
Arguments:
- tokens: bfloat16 [768, 8192], P(('rep', 'gx'), 'gy'), parts along dimension 0, may hold values from -6 to 6
- segment_ids: int32 [768], P(('rep', 'gx')), parts along dimension 0, may hold values from 0 to 1, as said below
- gate_weight: bfloat16 [8192, 2, 13312], P(None, 'gy', 'gx'), may hold values from -0.0625 to 0.0625
- up_weight: bfloat16 [8192, 2, 13312], P(None, 'gy', 'gx'), may hold values from -0.0625 to 0.0625
- down_weight: bfloat16 [2, 13312, 8192], P('gy', None, 'gx'), may hold values from -0.0390625 to 0.0390625
Outputs:
- grouped: bfloat16 [768, 8192], P(('rep', 'gx'), 'gy'), parts along dimension 0
There are 2 independent parts, one for each index of `rep`. A program takes and returns all parts, laid end to end along the dimension named above; an argument that names none is the same for every part. Nothing has to cross between parts.
Inputs may be any that keep to these rules, and one draw needn't show every extreme that they name: `segment_ids`: exactly 320 entries are 0 and 64 entries are 1.
All inputs are finite; a program needn't handle non-finite values.
Results may differ from a plain program's by a relative error of at most 0.0049.
Values may be sent and summed in bfloat16 or wider, within the bound.
A program may use at most 128 MiB of HBM per device.

v0:
```python
import jax
import jax.numpy as jnp
from jax import lax
from jax.sharding import PartitionSpec as P

PREFILL = 320


def grouped_target(token_kinds):
    decode_flag = token_kinds.astype(jnp.int32)
    prefill_flag = 1 - decode_flag
    prefill_rank = jnp.cumsum(prefill_flag) - 1
    decode_rank = jnp.cumsum(decode_flag) - 1
    return jnp.where(decode_flag == 0, prefill_rank, PREFILL + decode_rank)


def local(tokens, segment_ids, gate_weight, up_weight, down_weight):
    half_rows, token_kinds = (
        lax.all_gather(tokens, "gx", axis=0, tiled=True),
        lax.all_gather(segment_ids, "gx", axis=0, tiled=True),
    )
    gathered = lax.all_gather(half_rows, "gy", axis=1, tiled=True)
    gate_local = gate_weight.reshape(gate_weight.shape[0], -1)
    up_local = up_weight.reshape(up_weight.shape[0], -1)
    down_local = down_weight.reshape(-1, down_weight.shape[2])
    target = grouped_target(token_kinds)
    gate_value = jnp.dot(gathered, gate_local, preferred_element_type=jnp.float32)
    up_value = jnp.dot(gathered, up_local, preferred_element_type=jnp.float32)
    hidden = (jax.nn.silu(gate_value) * up_value).astype(jnp.bfloat16)
    partial_value = jnp.dot(
        lax.all_gather(hidden, "gx", axis=1, tiled=True),
        down_local,
        preferred_element_type=jnp.float32,
    )
    placed = jnp.zeros_like(partial_value).at[target].set(partial_value)
    switched = lax.all_to_all(placed, "gx", split_axis=0, concat_axis=1, tiled=True)
    return lax.psum_scatter(switched, "gy", scatter_dimension=1, tiled=True).astype(jnp.bfloat16)


def solution(mesh):
    placed = (
        P(("rep", "gx"), "gy"),
        P(("rep", "gx")),
        P(None, "gy", "gx"),
        P(None, "gy", "gx"),
        P("gy", None, "gx"),
    )
    return jax.shard_map(
        local, mesh=mesh, in_specs=placed, out_specs=P(("rep", "gx"), "gy"), check_vma=False
    )
```

profile of v0, /device:TPU:15, one launch (start us, length us, event | category | flops | bytes accessed | tf_op | source)
XLA Modules:
  0.0 348.1 jit_solution(17059045087787069002)
XLA Ops:
  6.5 0.7 all-gather.4.cloned.1.call-update
  7.3 0.0 all-gather.6.cloned.1.call-start
  7.3 61.0 %all-gather.4.cloned.1.call-done = bf16[384,4096]{1,0:T(8,128)(2,1)} async-done(((bf16[48,4096]{1,0:T(8,128)(2,1)}), bf16[384,4096]{1,0:T(8,128)(2,1)}) %all-gather.4.cloned.1.call-update) | async-done | bytes 3145744 | tf_op jit(solution)/shard_map/all_gather | solution.py:19
  68.3 0.0 all-gather.8.cloned.1.call-start
  68.3 20.0 %all-gather.6.cloned.1.call-done = bf16[384,8192]{1,0:T(8,128)(2,1)} async-done(((bf16[384,4096]{1,0:T(8,128)(2,1)}), bf16[384,8192]{1,0:T(8,128)(2,1)}) %all-gather.6.cloned.1.call-update) | async-done | bytes 6291472 | tf_op jit(solution)/shard_map/all_gather | solution.py:22
  88.4 17.7 %fusion.4 = f32[384,1664]{1,0:T(8,128)S(1)} fusion(bf16[384,8192]{1,0:T(8,128)(2,1)} %all-gather.6.cloned.1.call-done, bf16[8192,1,1664]{2,0,1:T(8,128)(2,1)} %param.7), kind=kOutput, calls=%fused_computation.5 | convolution fusion | flops 10468982784 | bytes 36110336 | tf_op jit(solution)/shard_map/dot_general | solution.py:27
  106.1 16.7 %fusion.9 = bf16[384,1664]{1,0:T(8,128)(2,1)} fusion(bf16[384,8192]{1,0:T(8,128)(2,1)S(1)} %copy-done, bf16[8192,1,1664]{2,0,1:T(8,128)(2,1)} %param.8, f32[384,1664]{1,0:T(8,128)S(1)} %fusion.4), kind=kOutput, calls=%fused_computation.8 | convolution fusion | flops 10472816640 | bytes 37388288 | tf_op jit(solution)/shard_map/dot_general | solution.py:28
  122.8 0.0 reduce-scatter.2.cloned.1.call-start
  122.9 0.6 dynamic-slice
  124.1 0.2 dynamic-update-slice
  124.4 7.5 %all-reduce = s32[384]{0:T(512)S(1)} all-reduce(s32[384]{0:T(512)S(1)} %dynamic-update-slice), channel_id=1, replica_groups=mesh['rep'=2,'gx'=8,'gy'=2] {'gx'}, use_global_device_ids=true, to_apply=%add | all-reduce | flops 384 | bytes 3072
  131.9 0.3 reduce-window.24
  132.2 0.1 slice.16
  132.3 0.3 reduce-window.16
  132.6 0.1 slice.14
  132.7 0.1 slice_reduce_fusion
  132.9 0.1 compare_select_fusion
  133.0 133.9 %all-gather.8.cloned.1.call-done = bf16[384,13312]{1,0:T(8,128)(2,1)} async-done(((bf16[384,1664]{1,0:T(8,128)(2,1)}), bf16[384,13312]{1,0:T(8,128)(2,1)}) %all-gather.8.cloned.1.call-update) | async-done | bytes 10223632 | tf_op jit(solution)/shard_map/all_gather | solution.py:31
  266.9 17.4 %fusion = f32[384,1024]{1,0:T(8,128)S(1)} fusion(bf16[384,13312]{1,0:T(8,128)(2,1)} %all-gather.8.cloned.1.call-done, bf16[1,13312,1024]{2,1,0:T(8,128)(2,1)} %param.9), kind=kOutput, calls=%fused_computation.1 | convolution fusion | flops 10468982784 | bytes 39059456 | tf_op jit(solution)/shard_map/dot_general | solution.py:30
  284.2 2.2 scatter_custom_fusion
  286.5 40.0 %all_to_all.19 = f32[8,48,1024]{2,1,0:T(8,128)S(1)} all-to-all(f32[8,48,1024]{2,1,0:T(8,128)S(1)} %bitcast.32), channel_id=1, replica_groups=mesh['rep'=2,'gx'=8,'gy'=2] {'gx'}, dimensions={0} | all-to-all | bytes 3145728 | tf_op jit(solution)/shard_map/all_to_all | solution.py:36
  326.5 1.3 copy.7
  327.8 11.8 %reduce-scatter.2.cloned.1.call-done = f32[48,4096]{1,0:T(8,128)} async-done(((f32[48,8192]{1,0:T(8,128)}), f32[48,4096]{1,0:T(8,128)}) %reduce-scatter.2.cloned.1.call-update) | async-done | bytes 786448 | tf_op jit(solution)/shard_map/reduce_scatter | solution.py:37
  339.6 1.9 convert_element_type.7
  (14 shorter events, 0.2 us)
Async XLA Ops:
  6.5 61.7 %all-gather.4.cloned.1.call-start = ((), (), s32[]{:S(2)}) async-start(), calls=%async_computation.2 | async-start | bytes 3538944 | tf_op jit(solution)/shard_map/all_gather | solution.py:19
  7.3 81.1 %all-gather.6.cloned.1.call-start = ((), (), s32[]{:S(2)}) async-start(), calls=%async_computation.3 | async-start | bytes 9437184 | tf_op jit(solution)/shard_map/all_gather | solution.py:22
  68.3 198.6 %all-gather.8.cloned.1.call-start = ((), (), s32[]{:S(2)}) async-start(), calls=%async_computation.4 | async-start | bytes 11501568 | tf_op jit(solution)/shard_map/all_gather | solution.py:31
  88.4 17.7 %copy-start = (bf16[384,8192]{1,0:T(8,128)(2,1)S(1)}, bf16[384,8192]{1,0:T(8,128)(2,1)}, u32[]{:S(2)}) copy-start(bf16[384,8192]{1,0:T(8,128)(2,1)} %all-gather.6.cloned.1.call-done) | copy-start | bytes 18874372
  106.1 16.8 %copy-start.2 = (u32[32]{0:T(128)S(1)}, u32[32]{0:T(128)}, u32[]{:S(2)}) copy-start(u32[32]{0:T(128)} %constant.26) | copy-start | bytes 388
  106.1 18.0 %copy-start.1 = (s32[48]{0:T(128)S(1)}, s32[48]{0:T(128)}, u32[]{:S(2)}) copy-start(s32[48]{0:T(128)} %param.6) | copy-start | bytes 580
  122.8 216.8 %reduce-scatter.2.cloned.1.call-start = ((), (), s32[]{:S(2)}) async-start(), calls=%async_computation.5 | async-start | bytes 2359296 | tf_op jit(solution)/shard_map/reduce_scatter | solution.py:37
Sparse Core Ops, SparseCore 0:
  9.5 58.7 all-gather.3
  69.8 18.5 all-gather.5
  122.9 143.9 all-gather.7
  327.9 11.6 reduce-scatter.1
where the time goes:
time: 349 us; the launch traced here: 348 us
  waiting for transfers between devices  227 us (65%)
  matrix products  51.7 us (15%)
  blocking collectives  47.6 us (14%)
  between operations  13.9 us (4%)
  local copies, waits for them, and re-layouts  4.61 us (1%)
    all_gather x1, waiting for transfers between devices, local(): lax.all_gather(hidden, 'gx', axis=1, tiled=True)  134 us
    all_gather x1, waiting for transfers between devices, local(): lax.all_gather(tokens, 'gx', axis=0, tiled=True)  61 us
    all_to_all x1, blocking collectives, local(): lax.all_to_all(placed, 'gx', split_axis=0, concat_axis=1, tiled=True)  40 us
    all_gather x1, waiting for transfers between devices, local(): gathered = lax.all_gather(half_rows, 'gy', axis=1, tiled=True)  20 us
    dot_general x1, matrix products, local(): jnp.dot(gathered, gate_local, preferred_element_type=jnp.float32)  17.7 us
    dot_general x1, matrix products, local(): jnp.dot(lax.all_gather(hidden, 'gx', axis=1, tiled=True), down_local, pre...  17.4 us
    dot_general x1, matrix products, local(): up_value = jnp.dot(gathered, up_local, preferred_element_type=jnp.float32)  16.7 us
    reduce_scatter x1, waiting for transfers between devices, local(): lax.psum_scatter(switched, 'gy', scatter_dimension=1, tiled=True)  11.8 us
  transfers between devices with their start and end apart: 4, of which 4 were waited for; matrix products, arithmetic and copies ran while one was open for 1% of the time, Pallas kernels for 0%

commit v1 on v0

--- a/solution.py
+++ b/solution.py
@@ -1,9 +1,18 @@
+import functools
+
 import jax
 import jax.numpy as jnp
 from jax import lax
+from jax.experimental import pallas as pl
+from jax.experimental.pallas import tpu as pltpu
 from jax.sharding import PartitionSpec as P
 
 PREFILL = 320
+MESH = pl.DeviceIdType.MESH
+LANES = 128
+W_SLOTS = 3
+TOKEN_MESSAGES = 4
+LAG1, LAG2, LAG3 = 2, 4, 6
 
 
 def grouped_target(token_kinds):
@@ -14,7 +23,7 @@
     return jnp.where(decode_flag == 0, prefill_rank, PREFILL + decode_rank)
 
 
-def local(tokens, segment_ids, gate_weight, up_weight, down_weight):
+def plain(tokens, segment_ids, gate_weight, up_weight, down_weight):
     half_rows, token_kinds = (
         lax.all_gather(tokens, "gx", axis=0, tiled=True),
         lax.all_gather(segment_ids, "gx", axis=0, tiled=True),
@@ -37,7 +46,389 @@
     return lax.psum_scatter(switched, "gy", scatter_dimension=1, tiled=True).astype(jnp.bfloat16)
 
 
+def kernel(
+    n, tokens, kinds, gate, up, down, out,
+    x, w, d, h, acc, other, kinds_all, place, stage, landed,
+    own_sem, w_sem, d_sem, kind_send, kind_recv,
+    t_send, t_recv, p_send, p_recv, h_send, h_recv,
+    a_send, a_recv, o_send, o_recv, o_local,
+):
+    rows, half = tokens.shape
+    total_rows = n * rows
+    chunks = h.shape[0]
+    local_units = chunks * LANES
+    rep, me, core = lax.axis_index("rep"), lax.axis_index("gx"), lax.axis_index("gy")
+    peer = 1 - core
+
+    def flip(g):
+        return g + 1 - 2 * lax.rem(g, 2)
+
+    xn = flip(me)
+    zp = lax.rem(me + 2, n)
+    zm = lax.rem(me + n - 2, n)
+    far = lax.rem(me + n // 2, n)
+
+    def w_load(c):
+        b = lax.rem(c, W_SLOTS)
+        cols = pl.ds(pl.multiple_of(c * LANES, LANES), LANES)
+        return [
+            pltpu.make_async_copy(ref.at[:, cols], w.at[b, :, pl.ds(i * LANES, LANES)], w_sem.at[b, i])
+            for i, ref in enumerate((gate, up))
+        ]
+
+    own_rows = pl.ds(pl.multiple_of(me * rows, rows), rows)
+    own_cols = pl.ds(pl.multiple_of(core * half, half), half)
+    own_copy = pltpu.make_async_copy(tokens, x.at[own_rows, own_cols], own_sem)
+    own_copy.start()
+    for c in range(W_SLOTS):
+        for copy in w_load(c):
+            copy.start()
+
+    barrier = pltpu.get_barrier_semaphore()
+    for step in range(n):
+        for k in range(2):
+            if step == 0 and k == 0:
+                continue
+            pl.semaphore_signal(
+                barrier, inc=1,
+                device_id=(rep, lax.rem(me + step, n), lax.rem(core + k, 2)), device_id_type=MESH,
+            )
+    pl.semaphore_wait(barrier, 2 * n - 1)
+
+    def remote(src, dst, send, recv, g, k):
+        return pltpu.make_async_remote_copy(
+            src_ref=src, dst_ref=dst, send_sem=send, recv_sem=recv,
+            device_id=(rep, g, k), device_id_type=MESH,
+        )
+
+    def regions(message):
+        ref = message["region"]
+        return [
+            (ref, xn, None), (ref, zm, None), (ref, zp, None),
+            (ref, far, 0), (ref, far, 1),
+            (ref, flip(zm), None), (ref, flip(zp), None),
+            (ref, flip(far), 0), (ref, flip(far), 1),
+        ]
+
+    def push(message, slot, src_g, part, to):
+        ref = message["region"](src_g, part)
+        remote(ref, ref, message["send"](slot), message["recv"](slot), to, core).start()
+
+    def take(message, slot):
+        fn, g, part = regions(message)[slot]
+        ref = fn(g, part)
+        remote(ref, ref, message["send"](slot), message["recv"](slot), me, core).wait_recv()
+        if message["arrived"] is not None:
+            message["arrived"](slot, ref)
+
+    def drain(message):
+        for slot, (fn, g, part) in enumerate(regions(message)):
+            ref = fn(g, part)
+            remote(ref, ref, message["send"](slot), message["recv"](slot), me, core).wait_send()
+
+    def stage0(message, kind):
+        push(message, 0, me, None, xn)
+        push(message, 1, me, None, zp)
+        push(message, 2, me, None, zm)
+
+    def stage1(message, kind):
+        if kind == 0:
+            take(message, 0)
+            push(message, 5, xn, None, zp)
+            push(message, 6, xn, None, zm)
+        take(message, 1)
+        push(message, 3, zm, 0, zp)
+        if kind == 1:
+            push(message, 5, zm, None, xn)
+        take(message, 2)
+        push(message, 4, zp, 1, zm)
+        if kind == 1:
+            push(message, 6, zp, None, xn)
+
+    def stage2(message, kind):
+        if kind == 0:
+            take(message, 5)
+            push(message, 7, flip(zm), 0, zp)
+            take(message, 6)
+            push(message, 8, flip(zp), 1, zm)
+        else:
+            take(message, 3)
+            push(message, 7, far, 0, xn)
+            take(message, 4)
+            push(message, 8, far, 1, xn)
+
+    def stage3(message, kind):
+        for slot in (3, 4, 7, 8) if kind == 0 else (0, 5, 6, 7, 8):
+            take(message, slot)
+
+    width = half // TOKEN_MESSAGES
+
+    def token_message(m):
+        def region(g, part):
+            start = core * half + m * width
+            size = width
+            if part is not None:
+                size = width // 2
+                start = start + part * size
+            return x.at[pl.ds(pl.multiple_of(g * rows, rows), rows), pl.ds(pl.multiple_of(start, LANES), size)]
+
+        def arrived(slot, ref):
+            remote(ref, ref, p_send.at[m, slot], p_recv.at[m, slot], me, peer).start()
+
+        return dict(
+            region=region, arrived=arrived,
+            send=lambda s: t_send.at[m, s], recv=lambda s: t_recv.at[m, s],
+        )
+
+    messages = [(token_message(m), m % 2) for m in range(TOKEN_MESSAGES)]
+    own_copy.wait()
+    for message, kind in messages:
+        stage0(message, kind)
+    own_ref = x.at[own_rows, own_cols]
+    own_push = remote(own_ref, own_ref, o_local.at[1], o_local.at[2], me, peer)
+    own_push.start()
+    kind_copies = []
+    for step in range(1, n):
+        g = lax.rem(me + step, n)
+        copy = remote(kinds, kinds_all.at[n - step], kind_send.at[step], kind_recv.at[n - step], g, core)
+        copy.start()
+        kind_copies.append(copy)
+
+    def d_start(i, carry):
+        c, g = i // n, lax.rem(i, n)
+        pltpu.make_async_copy(
+            down.at[pl.ds(pl.multiple_of(g * local_units + c * LANES, LANES), LANES), :],
+            d.at[c, pl.ds(pl.multiple_of(g * LANES, LANES), LANES), :],
+            d_sem.at[c],
+        ).start()
+        return carry
+
+    lax.fori_loop(0, chunks * n, d_start, 0)
+
+    for run in (stage1, stage2, stage3):
+        for message, kind in messages:
+            run(message, kind)
+    peer_cols = peer * half
+    remote(
+        own_ref, x.at[own_rows, pl.ds(pl.multiple_of(peer_cols, LANES), half)],
+        o_local.at[1], o_local.at[2], me, peer,
+    ).wait_recv()
+    for m, (message, kind) in enumerate(messages):
+        for slot, (fn, g, part) in enumerate(regions(message)):
+            start = peer_cols + m * width
+            size = width
+            if part is not None:
+                size = width // 2
+                start = start + part * size
+            dst = x.at[pl.ds(pl.multiple_of(g * rows, rows), rows), pl.ds(pl.multiple_of(start, LANES), size)]
+            remote(dst, dst, p_send.at[m, slot], p_recv.at[m, slot], me, peer).wait_recv()
+
+    def chunk_message(c):
+        def region(g, part):
+            cols = pl.ds(pl.multiple_of(g * LANES, LANES), LANES)
+            if part is None:
+                return h.at[c, :, cols]
+            size = total_rows // 2
+            return h.at[c, pl.ds(part * size, size), cols]
+
+        return dict(
+            region=region, arrived=None,
+            send=lambda s: h_send.at[c, s], recv=lambda s: h_recv.at[c, s],
+        )
+
+    def by_kind(c, fn):
+        for kind in range(2):
+            @pl.when(lax.rem(c, 2) == kind)
+            def _():
+                fn(chunk_message(c), kind)
+
+    acc[...] = jnp.zeros_like(acc)
+
+    def step_fn(t, carry):
+        @pl.when(t < chunks)
+        def _():
+            b = lax.rem(t, W_SLOTS)
+            for copy in w_load(t):
+                copy.wait()
+            both = jnp.dot(x[...], w[b], preferred_element_type=jnp.float32)
+            gate_value, up_value = both[:, :LANES], both[:, LANES:]
+            hidden = gate_value / (1.0 + jnp.exp(-gate_value)) * up_value
+            h[t, :, pl.ds(pl.multiple_of(me * LANES, LANES), LANES)] = hidden.astype(jnp.bfloat16)
+            stage0(chunk_message(t), 0)
+
+            @pl.when(t + W_SLOTS < chunks)
+            def _():
+                for copy in w_load(t + W_SLOTS):
+                    copy.start()
+
+        @pl.when((t >= LAG1) & (t < chunks + LAG1))
+        def _():
+            by_kind(t - LAG1, stage1)
+
+        @pl.when((t >= LAG2) & (t < chunks + LAG2))
+        def _():
+            by_kind(t - LAG2, stage2)
+
+        @pl.when(t >= LAG3)
+        def _():
+            c = t - LAG3
+            by_kind(c, stage3)
+            pltpu.make_async_copy(down.at[pl.ds(0, n * LANES), :], d.at[c], d_sem.at[c]).wait()
+            cut = acc.shape[2]
+            for j in range(2):
+                acc[j] += jnp.dot(
+                    h[c], d[c, :, j * cut : (j + 1) * cut], preferred_element_type=jnp.float32
+                )
+
+        @pl.when(t == chunks)
+        def _():
+            for i in range(1, n):
+                remote(kinds, kinds_all.at[i], kind_send.at[i], kind_recv.at[i], me, core).wait_recv()
+            flags = kinds[...]
+            for i in range(1, n):
+                flags = flags + kinds_all[i]
+            flags = flags.astype(jnp.float32)
+            shape = (total_rows, total_rows)
+            down_iota = lax.broadcasted_iota(jnp.int32, shape, 0)
+            lane_iota = lax.broadcasted_iota(jnp.int32, shape, 1)
+            upper = jnp.where(down_iota <= lane_iota, 1.0, 0.0).astype(jnp.bfloat16)
+            count = jnp.dot(flags.astype(jnp.bfloat16), upper, preferred_element_type=jnp.float32)
+            index = lax.broadcasted_iota(jnp.int32, flags.shape, 1).astype(jnp.float32)
+            target = jnp.where(flags == 0.0, index - count, PREFILL - 1.0 + count)
+            wanted = jnp.broadcast_to(target[0:1, :], shape)
+            place[...] = jnp.where(wanted == down_iota.astype(jnp.float32), 1.0, 0.0).astype(jnp.bfloat16)
+
+        return carry
+
+    lax.fori_loop(0, chunks + LAG3, step_fn, 0)
+
+    swap = remote(acc.at[peer], other, a_send, a_recv, me, peer)
+    swap.start()
+    swap.wait_recv()
+    summed = (acc[core] + other[...]).astype(jnp.bfloat16)
+    placed = jnp.dot(place[...], summed, preferred_element_type=jnp.float32).astype(jnp.bfloat16)
+    cut = acc.shape[2]
+    for g in range(n):
+        stage[g] = placed[g * rows : (g + 1) * rows]
+    quarter = n // 2
+    owner_core, position = me // quarter, lax.rem(me, quarter)
+    slot = position * 2 + core
+    cols = pl.ds(pl.multiple_of(slot * cut, cut), cut)
+    for step in range(1, n):
+        g = lax.rem(me + step, n)
+        remote(stage.at[g], landed.at[:, cols], o_send.at[step], o_recv.at[slot], g, owner_core).start()
+
+    @pl.when(core == owner_core)
+    def _():
+        copy = pltpu.make_async_copy(stage.at[me], out.at[:, cols], o_local.at[0])
+        copy.start()
+        copy.wait()
+
+    @pl.when(core != owner_core)
+    def _():
+        remote(stage.at[me], landed.at[:, cols], o_send.at[0], o_recv.at[slot], me, owner_core).start()
+
+    for s in range(n):
+        view = pl.ds(s * cut, cut)
+        from_g = core * quarter + s // 2
+        mine = (from_g == me) & (core == s % 2)
+
+        @pl.when(jnp.logical_not(mine))
+        def _():
+            remote(stage.at[0], landed.at[:, view], o_send.at[0], o_recv.at[s], me, core).wait_recv()
+            copy = pltpu.make_async_copy(landed.at[:, view], out.at[:, view], o_local.at[0])
+            copy.start()
+            copy.wait()
+
+    swap.wait_send()
+    own_push.wait_send()
+    for copy in kind_copies:
+        copy.wait_send()
+    for m, (message, kind) in enumerate(messages):
+        drain(message)
+        for s, (fn, g, part) in enumerate(regions(message)):
+            ref = fn(g, part)
+            remote(ref, ref, p_send.at[m, s], p_recv.at[m, s], me, peer).wait_send()
+
+    def drain_chunk(c, carry):
+        drain(chunk_message(c))
+        return carry
+
+    lax.fori_loop(0, chunks, drain_chunk, 0)
+    for step in range(1, n):
+        remote(stage.at[0], landed.at[:, cols], o_send.at[step], o_recv.at[slot], me, core).wait_send()
+
+    @pl.when(core != owner_core)
+    def _():
+        remote(stage.at[0], landed.at[:, cols], o_send.at[0], o_recv.at[slot], me, core).wait_send()
+
+
+def fused(n, tokens, segment_ids, gate_weight, up_weight, down_weight):
+    rows, half = tokens.shape
+    total_rows, width = n * rows, 2 * half
+    units = gate_weight.shape[2]
+    chunks = units // LANES
+    features = down_weight.shape[2]
+    me = lax.axis_index("gx")
+    kinds = lax.dynamic_update_slice(
+        jnp.zeros((8, total_rows), jnp.int32),
+        jnp.broadcast_to(segment_ids.astype(jnp.int32)[None], (8, rows)),
+        (0, me * rows),
+    )
+    cut = features // 2
+    dma = pltpu.SemaphoreType.DMA
+    any_spec = pl.BlockSpec(memory_space=pl.ANY)
+    return pl.pallas_call(
+        functools.partial(kernel, n),
+        out_shape=jax.ShapeDtypeStruct((rows, half), jnp.bfloat16),
+        in_specs=[any_spec, pl.BlockSpec(memory_space=pltpu.VMEM), any_spec, any_spec, any_spec],
+        out_specs=any_spec,
+        scratch_shapes=[
+            pltpu.VMEM((total_rows, width), jnp.bfloat16),
+            pltpu.VMEM((W_SLOTS, width, 2 * LANES), jnp.bfloat16),
+            pltpu.VMEM((chunks, n * LANES, features), jnp.bfloat16),
+            pltpu.VMEM((chunks, total_rows, n * LANES), jnp.bfloat16),
+            pltpu.VMEM((2, total_rows, cut), jnp.float32),
+            pltpu.VMEM((total_rows, cut), jnp.float32),
+            pltpu.VMEM((n, 8, total_rows), jnp.int32),
+            pltpu.VMEM((total_rows, total_rows), jnp.bfloat16),
+            pltpu.VMEM((n, rows, cut), jnp.bfloat16),
+            pltpu.VMEM((rows, half), jnp.bfloat16),
+            dma, dma((W_SLOTS, 2)), dma((chunks,)), dma((n,)), dma((n,)),
+            dma((TOKEN_MESSAGES, 9)), dma((TOKEN_MESSAGES, 9)),
+            dma((TOKEN_MESSAGES, 9)), dma((TOKEN_MESSAGES, 9)),
+            dma((chunks, 9)), dma((chunks, 9)),
+            dma, dma, dma((n,)), dma((n,)), dma((3,)),
+        ],
+        compiler_params=pltpu.CompilerParams(
+            collective_id=0, has_side_effects=True, vmem_limit_bytes=67_043_328
+        ),
+    )(
+        tokens, kinds, gate_weight.reshape(width, units), up_weight.reshape(width, units),
+        down_weight.reshape(n * units, features),
+    )
+
+
 def solution(mesh):
+    n = mesh.shape["gx"]
+
+    def local(tokens, segment_ids, gate_weight, up_weight, down_weight):
+        rows, half = tokens.shape
+        features = down_weight.shape[2]
+        fits = (
+            n == 8
+            and mesh.shape["gy"] == 2
+            and rows % 16 == 0
+            and (n * rows) % LANES == 0
+            and gate_weight.shape[2] % LANES == 0
+            and half % (2 * LANES * TOKEN_MESSAGES) == 0
+            and features % (2 * LANES) == 0
+            and features * n == 2 * half
+        )
+        if fits:
+            return fused(n, tokens, segment_ids, gate_weight, up_weight, down_weight)
+        return plain(tokens, segment_ids, gate_weight, up_weight, down_weight)
+
     placed = (
         P(("rep", "gx"), "gy"),
         P(("rep", "gx")),

time: 349 us -> 207 us (0.59)
  waiting for transfers between devices: 227 us -> 0 us
  Pallas kernels: 0 us -> 202 us
  matrix products: 51.7 us -> 0 us
  blocking collectives: 47.6 us -> 0 us
  between operations: 13.9 us -> 0.01 us
    all_gather x3 -> x0, waiting for transfers between devices: 215 us -> none  [the longest x1 134 us: local(): lax.all_gather(hidden, 'gx', axis=1, tiled=True)]
    pallas_call x0 -> x1, Pallas kernels: none -> 202 us  [fused(): pl.pallas_call(functools.partial(kernel, n), out_shape=jax.ShapeDtypeStru...]
    dot_general x3 -> x0, matrix products: 51.7 us -> none  [the longest x1 17.7 us: local(): jnp.dot(gathered, gate_local, preferred_element_type=jnp.float32)]
    all_to_all x1 -> x0, blocking collectives: 40 us -> none  [local(): lax.all_to_all(placed, 'gx', split_axis=0, concat_axis=1, tiled=True)]
    reduce_scatter x1 -> x0, waiting for transfers between devices: 11.8 us -> none  [local(): lax.psum_scatter(switched, 'gy', scatter_dimension=1, tiled=True)]
    unnamed x1 -> x0, blocking collectives: 7.52 us -> none
  transfers between devices with their start and end apart: 4 -> 0, of which waited for: 4 -> 0; matrix products, arithmetic and copies ran while one was open for 1% -> 0% of each run, Pallas kernels for 0% -> 0%
where the time goes in v1:
time: 207 us; the launch traced here: 206 us
  Pallas kernels  202 us (98%)
  local copies, waits for them, and re-layouts  4.46 us (2%)
    pallas_call x1, Pallas kernels, fused(): pl.pallas_call(functools.partial(kernel, n), out_shape=jax.ShapeDtypeStru...  202 us

profile of v1, /device:TPU:15, one launch (start us, length us, event | category | flops | bytes accessed | tf_op | source)
XLA Modules:
  0.0 206.4 jit_solution(100685778707110924)
XLA Ops:
  0.0 0.7 broadcast_in_dim.10
  0.7 0.6 broadcast_in_dim.4
  1.3 1.4 dynamic_update_slice.3.kinds
  2.7 201.9 %shard_map.55 = bf16[48,4096]{1,0:T(8,128)(2,1)} custom-call(bf16[48,4096]{1,0:T(8,128)(2,1)} %tokens.1, s32[8,384]{1,0:T(8,128)} %dynamic_update_slice.3.kinds, bf16[8192,1664]{1,0:T(8,128)(2,1)} %bitcast.3, bf16[8192,1664]{1,0:T(8,128)(2,1)} %bitcast.4, bf16[13312,1024]{1,0:T(8,128)(2,1)} %bitcast.5), custom_call_target="tpu_custom_call" | custom-call | tf_op jit(solution)/shard_map/pallas_call | solution.py:381
  204.6 1.8 copy.8
